TPU v7x, 32 devices: a whole 2x2x4 slice. The times are simulated.
32 devices in a mesh: seq: 16 (over z, y, core), slide: 2 (over x).
Axes of the slice: x: 2, y: 2, z: 4, core: 2. Of those that a mesh axis runs over, the one named last changes fastest.
Arguments:
- layer_input: bfloat16 [2, 4096, 768], P('slide', 'seq'), may hold values from -6 to 6
- cotangent: bfloat16 [2, 4096, 768], P('slide', 'seq'), may hold values from -6 to 6
- layer_norm_gain: float32 [768], replicated, may hold values from 0.25 to 1.75
- layer_norm_bias: float32 [768], replicated, may hold values from -3 to 3
- query_key_value_weight: bfloat16 [768, 2304], replicated, may hold values from -4 to 4
- output_weight: bfloat16 [768, 768], replicated, may hold values from -0.21875 to 0.21875
Outputs:
- layer_output: bfloat16 [2, 4096, 768], P('slide', 'seq')
- input_grad: bfloat16 [2, 4096, 768], P('slide', 'seq')
- grad_qkv: float32 [768, 2304], P('seq')
- grad_out: float32 [768, 768], P('seq')
- grad_gain: float32 [768], replicated
- grad_bias: float32 [768], replicated
All inputs are finite; a program needn't handle non-finite values.
Results may differ from a plain program's by a relative error of at most 0.011.
Values may be sent and summed in bfloat16 or wider, within the bound.
A program may use at most 128 MiB of HBM per device.

v0:
```python
import jax
import jax.numpy as jnp
from jax import lax
from jax.sharding import PartitionSpec as P

HEADS = 12
EPS = 1e-05


def from_behind(block, axis, distance):
    devices = range(lax.axis_size(axis))
    route = [(i - distance, i) for i in devices if i - distance in devices]
    return lax.ppermute(block, axis, route)


def apply_layer_norm(token_rows, scale_gain, shift_bias):
    values = token_rows.astype(jnp.float32)
    centered_rows = values - jnp.mean(values, axis=-1, keepdims=True)
    inverse_deviation = lax.rsqrt(
        jnp.mean(centered_rows * centered_rows, axis=-1, keepdims=True) + EPS
    )
    normalized_rows = centered_rows * inverse_deviation
    return (
        (normalized_rows * scale_gain + shift_bias).astype(jnp.bfloat16),
        normalized_rows,
        inverse_deviation,
    )


def attend(qkv_self, memory_key_value, memory_present):
    token_length = qkv_self.shape[0]
    feature_width = memory_key_value.shape[1] // 2
    head_dim = feature_width // HEADS
    query = qkv_self[:, :feature_width].reshape(token_length, HEADS, head_dim)
    keys = jnp.concatenate(
        [memory_key_value[:, :feature_width], qkv_self[:, feature_width : 2 * feature_width]], 0
    ).reshape(2 * token_length, HEADS, head_dim)
    values = jnp.concatenate(
        [memory_key_value[:, feature_width:], qkv_self[:, 2 * feature_width :]], 0
    ).reshape(2 * token_length, HEADS, head_dim)
    scores = jnp.einsum(
        "qhe,khe->hqk", query, keys, preferred_element_type=jnp.float32
    ) * head_dim ** (-0.5)
    row_ids = lax.broadcasted_iota(jnp.int32, (token_length, 2 * token_length), 0)
    col_ids = lax.broadcasted_iota(jnp.int32, (token_length, 2 * token_length), 1)
    allowed = jnp.where(col_ids < token_length, memory_present, col_ids - token_length <= row_ids)
    scores = jnp.where(allowed[None], scores, -1e30)
    top = jnp.max(scores, axis=-1, keepdims=True)
    weights = jnp.exp(scores - top)
    probs = weights / jnp.sum(weights, axis=-1, keepdims=True)
    probs_b = probs.astype(jnp.bfloat16)
    mixed = jnp.einsum("hqk,khe->qhe", probs_b, values, preferred_element_type=jnp.float32)
    mixed = mixed.reshape(token_length, feature_width).astype(jnp.bfloat16)
    return (mixed, probs, probs_b, query, keys, values)


def attend_back(d_mixed, probs, probs_b, query, keys, values):
    token_length, heads, head_dim = query.shape
    grad_heads = d_mixed.reshape(token_length, heads, head_dim)
    d_probs = jnp.einsum("qhe,khe->hqk", grad_heads, values, preferred_element_type=jnp.float32)
    d_scores = probs * (d_probs - jnp.sum(d_probs * probs, axis=-1, keepdims=True))
    d_scores_b = (d_scores * head_dim ** (-0.5)).astype(jnp.bfloat16)
    d_query = jnp.einsum("hqk,khe->qhe", d_scores_b, keys, preferred_element_type=jnp.float32)
    d_keys = jnp.einsum("hqk,qhe->khe", d_scores_b, query, preferred_element_type=jnp.float32)
    d_values = jnp.einsum("hqk,qhe->khe", probs_b, grad_heads, preferred_element_type=jnp.float32)
    return (
        d_query.reshape(token_length, -1).astype(jnp.bfloat16),
        d_keys.reshape(2 * token_length, -1).astype(jnp.bfloat16),
        d_values.reshape(2 * token_length, -1).astype(jnp.bfloat16),
    )


def block_forward(
    token_rows,
    gradient_list,
    current_query_key_value,
    memory_key_value,
    memory_present,
    current_normed,
    current_normalized,
    current_inverse_deviation,
    query_key_value_weight,
    output_weight,
    scale_gain,
):
    token_length = token_rows.shape[0]
    mixed, probs, probs_b, query, keys, values = attend(
        current_query_key_value, memory_key_value, memory_present
    )
    block_output = (
        token_rows.astype(jnp.float32)
        + jnp.dot(mixed, output_weight, preferred_element_type=jnp.float32)
    ).astype(jnp.bfloat16)
    d_mixed = jnp.dot(gradient_list, output_weight.T, preferred_element_type=jnp.float32).astype(
        jnp.bfloat16
    )
    grad_wout = jnp.dot(mixed.T, gradient_list, preferred_element_type=jnp.float32)
    d_query, d_keys, d_values = attend_back(d_mixed, probs, probs_b, query, keys, values)
    d_own = jnp.concatenate([d_query, d_keys[token_length:], d_values[token_length:]], 1)
    memory_gradient = jnp.concatenate([d_keys[:token_length], d_values[:token_length]], 1)
    grad_wqkv = jnp.dot(current_normed.T, d_own, preferred_element_type=jnp.float32)
    normed_gradient = jnp.dot(d_own, query_key_value_weight.T, preferred_element_type=jnp.float32)
    gain_gradient = jnp.sum(normed_gradient * current_normalized, axis=0)
    grad_b = jnp.sum(normed_gradient, axis=0)
    normalized_gradient = normed_gradient * scale_gain
    row_gradient = current_inverse_deviation * (
        normalized_gradient
        - jnp.mean(normalized_gradient, axis=-1, keepdims=True)
        - current_normalized
        * jnp.mean(normalized_gradient * current_normalized, axis=-1, keepdims=True)
    )
    input_gradient = (gradient_list.astype(jnp.float32) + row_gradient).astype(jnp.bfloat16)
    return (
        block_output,
        input_gradient,
        memory_gradient,
        (grad_wqkv, grad_wout, gain_gradient, grad_b),
    )


def memory_contributions(prior_normed, prior_normalized, memory_gradient, query_key_value_weight):
    feature_width = prior_normed.shape[1]
    key_value_gradient = jnp.dot(
        prior_normed.T, memory_gradient, preferred_element_type=jnp.float32
    )
    normed_gradient = jnp.dot(
        memory_gradient,
        query_key_value_weight[:, feature_width:].T,
        preferred_element_type=jnp.float32,
    )
    return (
        key_value_gradient,
        jnp.sum(normed_gradient * prior_normalized, axis=0),
        jnp.sum(normed_gradient, axis=0),
    )


def on_device(
    layer_input, cotangent, layer_norm_gain, layer_norm_bias, query_key_value_weight, output_weight
):
    token_rows = layer_input[0]
    gradient_list = cotangent[0]
    feature_width = token_rows.shape[1]
    normed_rows, normalized_rows, inverse_deviation = apply_layer_norm(
        token_rows, layer_norm_gain, layer_norm_bias
    )
    query_key_value = jnp.dot(
        normed_rows, query_key_value_weight, preferred_element_type=jnp.float32
    ).astype(jnp.bfloat16)
    has_first = lax.axis_index("seq") > 0
    previous_token_rows = from_behind(token_rows, "seq", 1)
    previous_normed_rows, previous_normalized, ignored_value = apply_layer_norm(
        previous_token_rows, layer_norm_gain, layer_norm_bias
    )
    kv_before = jnp.dot(
        previous_normed_rows,
        query_key_value_weight[:, feature_width:],
        preferred_element_type=jnp.float32,
    ).astype(jnp.bfloat16)
    block_output, input_gradient, memory_gradient, term_list = block_forward(
        token_rows,
        gradient_list,
        query_key_value,
        kv_before,
        has_first,
        normed_rows,
        normalized_rows,
        inverse_deviation,
        query_key_value_weight,
        output_weight,
        layer_norm_gain,
    )
    acc_qkv = term_list[0]
    acc_out = term_list[1]
    acc_gain = term_list[2]
    acc_bias = term_list[3]
    key_value_gradient, memory_gain, memory_bias = memory_contributions(
        previous_normed_rows, previous_normalized, memory_gradient, query_key_value_weight
    )
    acc_gain = acc_gain + memory_gain
    acc_bias = acc_bias + memory_bias
    combined = jnp.concatenate(
        [acc_qkv[:, :feature_width], acc_qkv[:, feature_width:] + key_value_gradient, acc_out], 1
    )
    seq_count = lax.axis_size("seq")
    slide_count = lax.axis_size("slide")
    factor = 1.0 / float(seq_count * slide_count * token_rows.shape[0]) ** 0.5
    gain_sum, bias_sum = lax.psum((acc_gain, acc_bias), ("seq", "slide"))
    shard = lax.psum_scatter(combined, "seq", scatter_dimension=0, tiled=True)
    shard = lax.psum(shard.astype(jnp.bfloat16), "slide").astype(jnp.float32)
    shard = shard * factor
    layer_output = block_output[None]
    input_grad = input_gradient[None]
    return (
        layer_output,
        input_grad,
        shard[:, : 3 * feature_width],
        shard[:, 3 * feature_width :],
        gain_sum * factor,
        bias_sum * factor,
    )


def solution(mesh):
    placed = (P("slide", "seq", None), P("slide", "seq", None), P(), P(), P(), P())
    return jax.shard_map(
        on_device,
        mesh=mesh,
        in_specs=placed,
        out_specs=(
            P("slide", "seq", None),
            P("slide", "seq", None),
            P("seq", None),
            P("seq", None),
            P(),
            P(),
        ),
        check_vma=False,
    )
```

profile of v0, /device:TPU:0, one launch (start us, length us, event | category | flops | bytes accessed | tf_op | source)
XLA Modules:
  0.0 261.9 jit_solution(17593352173310648972)
XLA Ops:
  7.2 2.6 collective-permute-start
  9.8 1.1 convert_reduce_fusion
  10.9 1.2 fusion.65
  12.2 3.4 %convolution_convert_fusion = bf16[256,2304]{1,0:T(8,128)(2,1)S(1)} fusion(bf16[768,2304]{1,0:T(8,128)(2,1)} %param.10, f32[256]{0:T(256)S(1)} %add_rsqrt_fusion, f32[256]{0:T(256)S(1)} %broadcast_multiply_fusion.4, f32[768]{0:T(1024)} %param.9, f32[768]{0:T(1024)} %param.8, bf16[1,256,768]{2,1,0:T(8,128)(2,1)} %param.6), kind=kOutput, calls=%fused_computation.10 | convolution fusion | flops 907739136 | bytes 5120000 | tf_op jit(solution)/shard_map/dot_general | solution.py:147
  15.7 1.3 convolution_convert_fusion.2
  17.5 1.2 copy.24
  19.6 1.4 fusion.69
  21.4 2.5 convolution_convert_fusion.1
  24.0 1.3 pad_maximum_fusion.2
  25.3 1.4 copy.21
  26.7 2.3 copy.23
  29.0 6.7 %fusion.95 = (f32[12,256]{1,0:T(8,128)}, f32[12,256,512]{2,1,0:T(8,128)}) fusion(pred[256,512]{1,0:T(8,128)(4,1)} %fusion.69, bf16[256,12,64]{0,2,1:T(8,128)(2,1)S(1)} %bitcast.71, bf16[512,12,64]{0,2,1:T(8,128)(2,1)} %bitcast.69), kind=kOutput, calls=%fused_computation.104 | convolution fusion | flops 207618560 | bytes 7614464 | tf_op jit(solution)/shard_map/sub | solution.py:49
  35.7 4.1 %fusion.37 = bf16[12,64,256]{2,1,0:T(8,128)(2,1)S(1)} fusion(bf16[512,12,64]{0,2,1:T(8,128)(2,1)S(1)} %bitcast.55, f32[12,256,512]{2,1,0:T(8,128)} %get-tuple-element.24, f32[12,256]{1,0:T(8,128)} %get-tuple-element.23), kind=kOutput, calls=%fused_computation.33 | convolution fusion | flops 204668928 | bytes 7483392 | tf_op jit(solution)/shard_map/hqk,khe->qhe/dot_general | solution.py:52
  40.3 1.7 fusion.30
  42.1 3.7 %fusion.96 = f32[12,256,512]{2,1,0:T(8,128)} fusion(bf16[256,12,64]{0,2,1:T(8,128)(2,1)S(1)} %bitcast.58, bf16[512,12,64]{0,2,1:T(8,128)(2,1)S(1)} %bitcast.56), kind=kOutput, calls=%fused_computation.105 | convolution fusion | flops 201326592 | bytes 7471104 | tf_op jit(solution)/shard_map/qhe,khe->hqk/dot_general | solution.py:60
  45.7 22.5 %fusion.40 = bf16[12,64,256]{2,1,0:T(8,128)(2,1)} fusion(bf16[512,12,64]{0,2,1:T(8,128)(2,1)} %bitcast.70, f32[12,256,512]{2,1,0:T(8,128)} %fusion.96, f32[12,256,512]{2,1,0:T(8,128)} %get-tuple-element.24, f32[12,256]{1,0:T(8,128)} %get-tuple-element.23), kind=kOutput, calls=%fused_computation.34 | convolution fusion | flops 212536832 | bytes 13774848 | tf_op jit(solution)/shard_map/hqk,khe->qhe/dot_general | solution.py:63
  68.2 25.9 %fusion.33 = bf16[512,12,64]{0,2,1:T(8,128)(2,1)} fusion(bf16[256,12,64]{0,2,1:T(8,128)(2,1)S(1)} %bitcast.72, f32[12,256,512]{2,1,0:T(8,128)} %fusion.96, f32[12,256,512]{2,1,0:T(8,128)} %get-tuple-element.24, f32[12,256]{1,0:T(8,128)S(1)} %copy-done.22), kind=kOutput, calls=%fused_computation.30 | convolution fusion | flops 212733440 | bytes 13774848 | tf_op jit(solution)/shard_map/hqk,qhe->khe/dot_general | solution.py:64
  94.1 1.3 fusion.93
  95.4 1.9 fusion.73
  97.4 1.3 fusion.70
  98.8 1.6 slice.80
  100.4 3.3 %slice_add_fusion = f32[768,1536]{1,0:T(8,128)} fusion(f32[768,2304]{1,0:T(8,128)S(1)} %fusion.70, bf16[256,768]{0,1:T(8,128)(2,1)S(1)} %bitcast.59, bf16[256,768]{0,1:T(8,128)(2,1)S(1)} %bitcast.61, bf16[256,768]{1,0:T(8,128)(2,1)S(1)} %collective-permute-done, f32[768]{0:T(1024)S(1)} %copy-done.13, f32[768]{0:T(1024)S(1)} %copy-done.12, ...), kind=kOutput, calls=%fused_computation.9 | convolution fusion | flops 607911936 | bytes 10625024 | tf_op jit(solution)/shard_map/dot_general | solution.py:123
  103.6 8.7 %pad_maximum_fusion = f32[768,3072]{1,0:T(8,128)} fusion(f32[768,768]{1,0:T(8,128)} %fusion.73, f32[768,1536]{1,0:T(8,128)} %slice_add_fusion, f32[768,768]{1,0:T(8,128)} %slice.80), kind=kLoop, calls=%fused_computation.2 | loop fusion | flops 4718592 | bytes 18874368 | tf_op jit(solution)/shard_map/concatenate | solution.py:182
  113.1 2.7 %fusion.90 = (f32[768]{0:T(1024)S(1)}, f32[768]{0:T(1024)S(1)}) fusion(f32[256]{0:T(256)} %copy-done.17, f32[256]{0:T(256)S(1)} %copy-done.16, bf16[256,768]{1,0:T(8,128)(2,1)S(1)} %collective-permute-done, bf16[768,2304]{1,0:T(8,128)(2,1)} %param.10, bf16[256,768]{0,1:T(8,128)(2,1)S(1)} %bitcast.60, bf16[256,768]{0,1:T(8,128)(2,1)S(1)} %bitcast.62), kind=kOutput, calls=%fused_computation.99 | convolution fusion | flops 606730752 | bytes 3547136 | tf_op jit(solution)/shard_map/dot_general | solution.py:126
  116.1 1.4 fusion.64
  117.6 43.3 %all-reduce = (f32[768]{0:T(1024)S(1)}, f32[768]{0:T(1024)S(1)}) all-reduce(f32[768]{0:T(1024)S(1)} %add.62, f32[768]{0:T(1024)S(1)} %add.63), channel_id=1, replica_groups=mesh['seq'=16,'slide'=2] {'seq','slide'}, use_global_device_ids=true, to_apply=%region_13.14 | all-reduce | flops 1536 | bytes 12288 | tf_op jit(solution)/shard_map/psum | solution.py:188
  162.1 64.4 %reduce-scatter.2.cloned.1.call-done = f32[48,3072]{1,0:T(8,128)} async-done(((f32[768,3072]{1,0:T(8,128)}), f32[48,3072]{1,0:T(8,128)}) %reduce-scatter.2.cloned.1.call-update) | async-done | bytes 589840 | tf_op jit(solution)/shard_map/reduce_scatter | solution.py:189
  226.4 1.8 convert_element_type.99
  228.2 1.3 fusion.43
  229.5 1.1 fusion.72
  230.6 22.1 %all-reduce.3.cloned.1.call-done = bf16[48,3072]{1,0:T(8,128)(2,1)} async-done(((bf16[48,3072]{1,0:T(8,128)(2,1)}), bf16[48,3072]{1,0:T(8,128)(2,1)}) %all-reduce.3.cloned.1.call-update) | async-done | bytes 294928 | tf_op jit(solution)/shard_map/psum | solution.py:190
  252.6 1.0 convert_multiply_fusion
  (71 shorter events, 6.4 us)
Async XLA Ops:
  7.2 8.5 %copy-start = (bf16[768,768]{1,0:T(8,128)(2,1)S(1)}, bf16[768,768]{1,0:T(8,128)(2,1)}, u32[]{:S(2)}) copy-start(bf16[768,768]{1,0:T(8,128)(2,1)} %param.11) | copy-start | bytes 3538948
  7.2 219.2 %reduce-scatter.2.cloned.1.call-start = ((), (), s32[]{:S(2)}) async-start(), calls=%async_computation.1 | async-start | bytes 10027008 | tf_op jit(solution)/shard_map/reduce_scatter | solution.py:189
  7.2 13.7 %collective-permute-start = (bf16[256,768]{1,0:T(8,128)(2,1)}, bf16[256,768]{1,0:T(8,128)(2,1)S(1)}, u32[]{:S(2)}, u32[]{:S(2)}) collective-permute-start(bf16[256,768]{1,0:T(8,128)(2,1)} %bitcast.54), channel_id=1, source_target_pairs={{0,2},{2,4},{4,6},{6,8},{8,10},{10,12},{12,14},{14,16},{16,18},{18... | collective-permute-start | bytes 1179656 | tf_op jit(solution)/shard_map/ppermute | solution.py:13
  12.2 3.5 %copy-start.2 = (bf16[1,256,768]{2,1,0:T(8,128)(2,1)S(1)}, bf16[1,256,768]{2,1,0:T(8,128)(2,1)}, u32[]{:S(2)}) copy-start(bf16[1,256,768]{2,1,0:T(8,128)(2,1)} %param.7) | copy-start | bytes 1179652
  15.6 5.8 %copy-start.12 = (f32[768]{0:T(1024)S(1)}, f32[768]{0:T(1024)}, u32[]{:S(2)}) copy-start(f32[768]{0:T(1024)} %param.8) | copy-start | bytes 9220
  15.6 5.8 %copy-start.13 = (f32[768]{0:T(1024)S(1)}, f32[768]{0:T(1024)}, u32[]{:S(2)}) copy-start(f32[768]{0:T(1024)} %param.9) | copy-start | bytes 9220
  21.1 2.8 %copy-start.14 = (f32[256]{0:T(256)}, f32[256]{0:T(256)S(1)}, u32[]{:S(2)}) copy-start(f32[256]{0:T(256)S(1)} %broadcast_multiply_fusion.5) | copy-start | bytes 3076
  21.4 2.6 copy-start.17
  24.0 5.0 %copy-start.8 = (bf16[256,768]{0,1:T(8,128)(2,1)S(1)}, bf16[256,768]{0,1:T(8,128)(2,1)}, u32[]{:S(2)}) copy-start(bf16[256,768]{0,1:T(8,128)(2,1)} %copy.22) | copy-start | bytes 1179652
  35.7 4.6 %copy-start.20 = (f32[12,256,512]{2,1,0:T(8,128)S(1)}, f32[12,256,512]{2,1,0:T(8,128)}, u32[]{:S(2)}) copy-start(f32[12,256,512]{2,1,0:T(8,128)} %get-tuple-element.24) | copy-start | bytes 18874372
  35.7 4.6 %copy-start.21 = (f32[12,256]{1,0:T(8,128)S(1)}, f32[12,256]{1,0:T(8,128)}, u32[]{:S(2)}) copy-start(f32[12,256]{1,0:T(8,128)} %get-tuple-element.23) | copy-start | bytes 36868
  45.7 22.5 %copy-start.9 = (bf16[256,768]{0,1:T(8,128)(2,1)S(1)}, bf16[256,768]{0,1:T(8,128)(2,1)}, u32[]{:S(2)}) copy-start(bf16[256,768]{0,1:T(8,128)(2,1)} %copy.22) | copy-start | bytes 1179652
  45.7 22.5 %copy-start.22 = (f32[12,256]{1,0:T(8,128)S(1)}, f32[12,256]{1,0:T(8,128)}, u32[]{:S(2)}) copy-start(f32[12,256]{1,0:T(8,128)} %get-tuple-element.23) | copy-start | bytes 36868
  94.1 3.2 %copy-start.7 = (bf16[512,12,64]{0,2,1:T(8,128)(2,1)S(1)}, bf16[512,12,64]{0,2,1:T(8,128)(2,1)}, u32[]{:S(2)}) copy-start(bf16[512,12,64]{0,2,1:T(8,128)(2,1)} %fusion.33) | copy-start | bytes 2359300
  94.1 3.3 %copy-start.1 = (bf16[1,256,768]{2,1,0:T(8,128)(2,1)S(1)}, bf16[1,256,768]{2,1,0:T(8,128)(2,1)}, u32[]{:S(2)}) copy-start(bf16[1,256,768]{2,1,0:T(8,128)(2,1)} %param.6) | copy-start | bytes 1179652
  94.1 3.3 %copy-start.10 = (bf16[12,64,256]{2,1,0:T(8,128)(2,1)S(1)}, bf16[12,64,256]{2,1,0:T(8,128)(2,1)}, u32[]{:S(2)}) copy-start(bf16[12,64,256]{2,1,0:T(8,128)(2,1)} %fusion.40) | copy-start | bytes 1179652
  95.4 3.3 %copy-start.3 = (bf16[256,12,64]{0,2,1:T(8,128)(2,1)}, bf16[256,12,64]{0,2,1:T(8,128)(2,1)S(1)}, u32[]{:S(2)}) copy-start(bf16[256,12,64]{0,2,1:T(8,128)(2,1)S(1)} %get-tuple-element.20) | copy-start | bytes 1179652
  97.4 1.4 copy-start.5
  98.8 1.6 copy-start.15
  98.8 1.6 copy-start.18
  112.4 0.7 copy-start.16
  112.4 140.2 %all-reduce.3.cloned.1.call-start = ((), (), s32[]{:S(2)}) async-start(), calls=%async_computation.2 | async-start | bytes 589824 | tf_op jit(solution)/shard_map/psum | solution.py:190
  113.0 2.7 %copy-start.4 = (bf16[256,12,64]{0,2,1:T(8,128)(2,1)S(1)}, bf16[256,12,64]{0,2,1:T(8,128)(2,1)}, u32[]{:S(2)}) copy-start(bf16[256,12,64]{0,2,1:T(8,128)(2,1)} %copy-done.3) | copy-start | bytes 1179652
  113.1 2.7 %copy-start.6 = (bf16[256,12,64]{0,2,1:T(8,128)(2,1)S(1)}, bf16[256,12,64]{0,2,1:T(8,128)(2,1)}, u32[]{:S(2)}) copy-start(bf16[256,12,64]{0,2,1:T(8,128)(2,1)} %copy-done.5) | copy-start | bytes 1179652
  113.1 2.7 %copy-start.11 = (bf16[12,64,256]{2,1,0:T(8,128)(2,1)S(1)}, bf16[12,64,256]{2,1,0:T(8,128)(2,1)}, u32[]{:S(2)}) copy-start(bf16[12,64,256]{2,1,0:T(8,128)(2,1)} %fusion.40) | copy-start | bytes 1179652
  113.1 3.1 %copy-start.19 = (bf16[768,2304]{1,0:T(8,128)(2,1)S(1)}, bf16[768,2304]{1,0:T(8,128)(2,1)}, u32[]{:S(2)}) copy-start(bf16[768,2304]{1,0:T(8,128)(2,1)} %param.10) | copy-start | bytes 10616836
Sparse Core Ops, SparseCore 0:
  112.5 113.8 reduce-scatter.1
  229.3 23.3 all-reduce.2
where the time goes:
time: 263 us; the launch traced here: 262 us
  waiting for transfers between devices  86.4 us (33%)
  matrix products  83.5 us (32%)
  blocking collectives  43.3 us (16%)
  other arithmetic  19.8 us (8%)
  between operations  14.4 us (5%)
  local copies, waits for them, and re-layouts  11.9 us (5%)
  starting transfers between devices  2.63 us (1%)
    reduce_scatter x1, waiting for transfers between devices, on_device(): shard = lax.psum_scatter(combined, 'seq', scatter_dimension=0, tiled=True)  64.4 us
    psum x1, blocking collectives, on_device(): gain_sum, bias_sum = lax.psum((acc_gain, acc_bias), ('seq', 'slide'))  43.3 us
    dot_general x1, matrix products, attend_back(): jnp.einsum('hqk,qhe->khe', d_scores_b, query, preferred_element_type=jnp....  25.9 us
    dot_general x1, matrix products, attend_back(): jnp.einsum('hqk,khe->qhe', d_scores_b, keys, preferred_element_type=jnp.f...  22.5 us
    psum x1, waiting for transfers between devices, on_device(): shard = lax.psum(shard.astype(jnp.bfloat16), 'slide').astype(jnp.float32)  22.1 us
    concatenate x1, other arithmetic, on_device(): jnp.concatenate([acc_qkv[:, :feature_width], acc_qkv[:, feature_width:] +...  8.74 us
    sub x1, matrix products, attend(): weights = jnp.exp(scores - top)  6.67 us
  transfers between devices with their start and end apart: 3, of which 2 were waited for; matrix products, arithmetic and copies ran while one was open for 7% of the time, Pallas kernels for 0%

commit v1 on v0

--- a/solution.py
+++ b/solution.py
@@ -187,7 +187,7 @@
     factor = 1.0 / float(seq_count * slide_count * token_rows.shape[0]) ** 0.5
     gain_sum, bias_sum = lax.psum((acc_gain, acc_bias), ("seq", "slide"))
     shard = lax.psum_scatter(combined, "seq", scatter_dimension=0, tiled=True)
-    shard = lax.psum(shard.astype(jnp.bfloat16), "slide").astype(jnp.float32)
+    shard = jnp.sum(lax.all_gather(shard.astype(jnp.bfloat16), "slide"), axis=0).astype(jnp.float32)
     shard = shard * factor
     layer_output = block_output[None]
     input_grad = input_gradient[None]

time: 263 us -> 246 us (0.935)
  waiting for transfers between devices: 86.4 us -> 63 us
  blocking collectives: 43.3 us -> 51.5 us
    psum x1 -> x0, waiting for transfers between devices: 22.1 us -> none  [on_device(): shard = lax.psum(shard.astype(jnp.bfloat16), 'slide').astype(jnp.float32)]
    all_gather x0 -> x1, blocking collectives: none -> 9.12 us  [on_device(): lax.all_gather(shard.astype(jnp.bfloat16), 'slide')]
  transfers between devices with their start and end apart: 3 -> 2, of which waited for: 2 -> 1; matrix products, arithmetic and copies ran while one was open for 7% -> 8% of each run, Pallas kernels for 0% -> 0%
where the time goes in v1:
time: 246 us; the launch traced here: 245 us
  matrix products  83.5 us (34%)
  waiting for transfers between devices  63 us (26%)
  blocking collectives  51.5 us (21%)
  other arithmetic  18.3 us (7%)
  between operations  14.4 us (6%)
  local copies, waits for them, and re-layouts  11.9 us (5%)
  starting transfers between devices  2.59 us (1%)
    reduce_scatter x1, waiting for transfers between devices, on_device(): shard = lax.psum_scatter(combined, 'seq', scatter_dimension=0, tiled=True)  63 us
    psum x1, blocking collectives, on_device(): gain_sum, bias_sum = lax.psum((acc_gain, acc_bias), ('seq', 'slide'))  42.3 us
    dot_general x1, matrix products, attend_back(): jnp.einsum('hqk,qhe->khe', d_scores_b, query, preferred_element_type=jnp....  25.9 us
    dot_general x1, matrix products, attend_back(): jnp.einsum('hqk,khe->qhe', d_scores_b, keys, preferred_element_type=jnp.f...  22.5 us
    all_gather x1, blocking collectives, on_device(): lax.all_gather(shard.astype(jnp.bfloat16), 'slide')  9.12 us
    concatenate x1, other arithmetic, on_device(): jnp.concatenate([acc_qkv[:, :feature_width], acc_qkv[:, feature_width:] +...  8.74 us
    sub x1, matrix products, attend(): weights = jnp.exp(scores - top)  6.67 us
  transfers between devices with their start and end apart: 2, of which 1 were waited for; matrix products, arithmetic and copies ran while one was open for 8% of the time, Pallas kernels for 0%

profile of v1, /device:TPU:0, one launch (start us, length us, event | category | flops | bytes accessed | tf_op | source)
XLA Modules:
  0.0 245.2 jit_solution(12407373695497252435)
XLA Ops:
  7.2 2.6 %collective-permute-start = (bf16[256,768]{1,0:T(8,128)(2,1)}, bf16[256,768]{1,0:T(8,128)(2,1)S(1)}, u32[]{:S(2)}, u32[]{:S(2)}) collective-permute-start(bf16[256,768]{1,0:T(8,128)(2,1)} %bitcast.55), channel_id=1, source_target_pairs={{0,2},{2,4},{4,6},{6,8},{8,10},{10,12},{12,14},{14,16},{16,18},{18... | collective-permute-start | bytes 1179656 | tf_op jit(solution)/shard_map/ppermute | solution.py:13
  9.8 1.1 convert_reduce_fusion
  10.9 1.2 fusion.65
  12.2 3.4 %convolution_convert_fusion = bf16[256,2304]{1,0:T(8,128)(2,1)S(1)} fusion(bf16[768,2304]{1,0:T(8,128)(2,1)} %param.10, f32[256]{0:T(256)S(1)} %add_rsqrt_fusion, f32[256]{0:T(256)S(1)} %broadcast_multiply_fusion.4, f32[768]{0:T(1024)} %param.9, f32[768]{0:T(1024)} %param.8, bf16[1,256,768]{2,1,0:T(8,128)(2,1)} %param.6), kind=kOutput, calls=%fused_computation.10 | convolution fusion | flops 907739136 | bytes 5120000 | tf_op jit(solution)/shard_map/dot_general | solution.py:147
  15.7 1.3 convolution_convert_fusion.2
  17.5 1.2 copy.24
  18.6 0.9 copy.22
  19.6 1.4 fusion.69
  21.4 2.5 %convolution_convert_fusion.1 = bf16[256,1536]{1,0:T(8,128)(2,1)S(1)} fusion(bf16[768,2304]{1,0:T(8,128)(2,1)} %param.10, bf16[256,768]{1,0:T(8,128)(2,1)S(1)} %collective-permute-done, f32[768]{0:T(1024)S(1)} %copy-done.13, f32[768]{0:T(1024)S(1)} %copy-done.12, f32[256]{0:T(256)S(1)} %add_rsqrt_fusion.1, f32[256]{0:T(256)S(1)} %broadcast_multiply_fusion.5), kind=kOutput, calls=%fused_computation.19 | convolution fusion | flops 605552640 | bytes 3547136 | tf_op jit(solution)/shard_map/dot_general | solution.py:155
  24.0 1.3 pad_maximum_fusion.2
  25.3 1.4 copy.21
  26.7 2.3 copy.23
  29.0 6.7 %fusion.95 = (f32[12,256]{1,0:T(8,128)}, f32[12,256,512]{2,1,0:T(8,128)}) fusion(pred[256,512]{1,0:T(8,128)(4,1)} %fusion.69, bf16[256,12,64]{0,2,1:T(8,128)(2,1)S(1)} %bitcast.73, bf16[512,12,64]{0,2,1:T(8,128)(2,1)} %bitcast.71), kind=kOutput, calls=%fused_computation.104 | convolution fusion | flops 207618560 | bytes 7614464 | tf_op jit(solution)/shard_map/sub | solution.py:49
  35.7 4.1 %fusion.37 = bf16[12,64,256]{2,1,0:T(8,128)(2,1)S(1)} fusion(bf16[512,12,64]{0,2,1:T(8,128)(2,1)S(1)} %bitcast.56, f32[12,256,512]{2,1,0:T(8,128)} %get-tuple-element.24, f32[12,256]{1,0:T(8,128)} %get-tuple-element.23), kind=kOutput, calls=%fused_computation.33 | convolution fusion | flops 204668928 | bytes 7483392 | tf_op jit(solution)/shard_map/hqk,khe->qhe/dot_general | solution.py:52
  40.3 1.7 fusion.30
  42.1 3.7 %fusion.96 = f32[12,256,512]{2,1,0:T(8,128)} fusion(bf16[256,12,64]{0,2,1:T(8,128)(2,1)S(1)} %bitcast.60, bf16[512,12,64]{0,2,1:T(8,128)(2,1)S(1)} %bitcast.57), kind=kOutput, calls=%fused_computation.105 | convolution fusion | flops 201326592 | bytes 7471104 | tf_op jit(solution)/shard_map/qhe,khe->hqk/dot_general | solution.py:60
  45.7 22.5 %fusion.40 = bf16[12,64,256]{2,1,0:T(8,128)(2,1)} fusion(bf16[512,12,64]{0,2,1:T(8,128)(2,1)} %bitcast.72, f32[12,256,512]{2,1,0:T(8,128)} %fusion.96, f32[12,256,512]{2,1,0:T(8,128)} %get-tuple-element.24, f32[12,256]{1,0:T(8,128)} %get-tuple-element.23), kind=kOutput, calls=%fused_computation.34 | convolution fusion | flops 212536832 | bytes 13774848 | tf_op jit(solution)/shard_map/hqk,khe->qhe/dot_general | solution.py:63
  68.2 25.9 %fusion.33 = bf16[512,12,64]{0,2,1:T(8,128)(2,1)} fusion(bf16[256,12,64]{0,2,1:T(8,128)(2,1)S(1)} %bitcast.74, f32[12,256,512]{2,1,0:T(8,128)} %fusion.96, f32[12,256,512]{2,1,0:T(8,128)} %get-tuple-element.24, f32[12,256]{1,0:T(8,128)S(1)} %copy-done.22), kind=kOutput, calls=%fused_computation.30 | convolution fusion | flops 212733440 | bytes 13774848 | tf_op jit(solution)/shard_map/hqk,qhe->khe/dot_general | solution.py:64
  94.1 1.3 fusion.93
  95.4 1.9 fusion.73
  97.4 1.3 fusion.70
  98.8 1.6 slice.80
  100.4 3.3 %slice_add_fusion = f32[768,1536]{1,0:T(8,128)} fusion(f32[768,2304]{1,0:T(8,128)S(1)} %fusion.70, bf16[256,768]{0,1:T(8,128)(2,1)S(1)} %bitcast.61, bf16[256,768]{0,1:T(8,128)(2,1)S(1)} %bitcast.63, bf16[256,768]{1,0:T(8,128)(2,1)S(1)} %collective-permute-done, f32[768]{0:T(1024)S(1)} %copy-done.13, f32[768]{0:T(1024)S(1)} %copy-done.12, ...), kind=kOutput, calls=%fused_computation.9 | convolution fusion | flops 607911936 | bytes 10625024 | tf_op jit(solution)/shard_map/dot_general | solution.py:123
  103.6 8.7 %pad_maximum_fusion = f32[768,3072]{1,0:T(8,128)} fusion(f32[768,768]{1,0:T(8,128)} %fusion.73, f32[768,1536]{1,0:T(8,128)} %slice_add_fusion, f32[768,768]{1,0:T(8,128)} %slice.80), kind=kLoop, calls=%fused_computation.2 | loop fusion | flops 4718592 | bytes 18874368 | tf_op jit(solution)/shard_map/concatenate | solution.py:182
  113.1 2.7 %fusion.90 = (f32[768]{0:T(1024)S(1)}, f32[768]{0:T(1024)S(1)}) fusion(f32[256]{0:T(256)} %copy-done.17, f32[256]{0:T(256)S(1)} %copy-done.16, bf16[256,768]{1,0:T(8,128)(2,1)S(1)} %collective-permute-done, bf16[768,2304]{1,0:T(8,128)(2,1)} %param.10, bf16[256,768]{0,1:T(8,128)(2,1)S(1)} %bitcast.62, bf16[256,768]{0,1:T(8,128)(2,1)S(1)} %bitcast.64), kind=kOutput, calls=%fused_computation.99 | convolution fusion | flops 606730752 | bytes 3547136 | tf_op jit(solution)/shard_map/dot_general | solution.py:126
  116.1 1.4 fusion.64
  117.6 42.3 %all-reduce = (f32[768]{0:T(1024)S(1)}, f32[768]{0:T(1024)S(1)}) all-reduce(f32[768]{0:T(1024)S(1)} %add.60, f32[768]{0:T(1024)S(1)} %add.61), channel_id=1, replica_groups=mesh['seq'=16,'slide'=2] {'seq','slide'}, use_global_device_ids=true, to_apply=%region_13.14 | all-reduce | flops 1536 | bytes 12288 | tf_op jit(solution)/shard_map/psum | solution.py:188
  159.9 1.3 fusion.43
  162.4 1.1 fusion.72
  163.4 63.0 %reduce-scatter.2.cloned.1.call-done = f32[48,3072]{1,0:T(8,128)} async-done(((f32[768,3072]{1,0:T(8,128)}), f32[48,3072]{1,0:T(8,128)}) %reduce-scatter.2.cloned.1.call-update) | async-done | bytes 589840 | tf_op jit(solution)/shard_map/reduce_scatter | solution.py:189
  226.4 1.1 convert_element_type.101
  227.5 9.1 %all-gather = bf16[96,3072]{1,0:T(8,128)(2,1)S(1)} all-gather(bf16[48,3072]{1,0:T(8,128)(2,1)S(1)} %convert_element_type.101), channel_id=2, replica_groups=mesh['seq'=16,'slide'=2] {'slide'}, dimensions={0}, use_global_device_ids=true | all-gather | bytes 884736 | tf_op jit(solution)/shard_map/all_gather | solution.py:190
  (70 shorter events, 5.7 us)
Async XLA Ops:
  7.2 8.5 %copy-start = (bf16[768,768]{1,0:T(8,128)(2,1)S(1)}, bf16[768,768]{1,0:T(8,128)(2,1)}, u32[]{:S(2)}) copy-start(bf16[768,768]{1,0:T(8,128)(2,1)} %param.11) | copy-start | bytes 3538948
  7.2 219.2 %reduce-scatter.2.cloned.1.call-start = ((), (), s32[]{:S(2)}) async-start(), calls=%async_computation.1 | async-start | bytes 10027008 | tf_op jit(solution)/shard_map/reduce_scatter | solution.py:189
  7.2 13.7 %collective-permute-start = (bf16[256,768]{1,0:T(8,128)(2,1)}, bf16[256,768]{1,0:T(8,128)(2,1)S(1)}, u32[]{:S(2)}, u32[]{:S(2)}) collective-permute-start(bf16[256,768]{1,0:T(8,128)(2,1)} %bitcast.55), channel_id=1, source_target_pairs={{0,2},{2,4},{4,6},{6,8},{8,10},{10,12},{12,14},{14,16},{16,18},{18... | collective-permute-start | bytes 1179656 | tf_op jit(solution)/shard_map/ppermute | solution.py:13
  12.2 3.5 %copy-start.2 = (bf16[1,256,768]{2,1,0:T(8,128)(2,1)S(1)}, bf16[1,256,768]{2,1,0:T(8,128)(2,1)}, u32[]{:S(2)}) copy-start(bf16[1,256,768]{2,1,0:T(8,128)(2,1)} %param.7) | copy-start | bytes 1179652
  15.6 5.8 %copy-start.12 = (f32[768]{0:T(1024)S(1)}, f32[768]{0:T(1024)}, u32[]{:S(2)}) copy-start(f32[768]{0:T(1024)} %param.8) | copy-start | bytes 9220
  15.6 5.8 %copy-start.13 = (f32[768]{0:T(1024)S(1)}, f32[768]{0:T(1024)}, u32[]{:S(2)}) copy-start(f32[768]{0:T(1024)} %param.9) | copy-start | bytes 9220
  21.1 2.8 %copy-start.14 = (f32[256]{0:T(256)}, f32[256]{0:T(256)S(1)}, u32[]{:S(2)}) copy-start(f32[256]{0:T(256)S(1)} %broadcast_multiply_fusion.5) | copy-start | bytes 3076
  21.4 2.6 %copy-start.17 = (f32[256]{0:T(256)}, f32[256]{0:T(256)S(1)}, u32[]{:S(2)}) copy-start(f32[256]{0:T(256)S(1)} %add_rsqrt_fusion.1) | copy-start | bytes 3076
  24.0 5.0 %copy-start.8 = (bf16[256,768]{0,1:T(8,128)(2,1)S(1)}, bf16[256,768]{0,1:T(8,128)(2,1)}, u32[]{:S(2)}) copy-start(bf16[256,768]{0,1:T(8,128)(2,1)} %copy.22) | copy-start | bytes 1179652
  35.7 4.6 %copy-start.20 = (f32[12,256,512]{2,1,0:T(8,128)S(1)}, f32[12,256,512]{2,1,0:T(8,128)}, u32[]{:S(2)}) copy-start(f32[12,256,512]{2,1,0:T(8,128)} %get-tuple-element.24) | copy-start | bytes 18874372
  35.7 4.6 %copy-start.21 = (f32[12,256]{1,0:T(8,128)S(1)}, f32[12,256]{1,0:T(8,128)}, u32[]{:S(2)}) copy-start(f32[12,256]{1,0:T(8,128)} %get-tuple-element.23) | copy-start | bytes 36868
  45.7 22.5 %copy-start.9 = (bf16[256,768]{0,1:T(8,128)(2,1)S(1)}, bf16[256,768]{0,1:T(8,128)(2,1)}, u32[]{:S(2)}) copy-start(bf16[256,768]{0,1:T(8,128)(2,1)} %copy.22) | copy-start | bytes 1179652
  45.7 22.5 %copy-start.22 = (f32[12,256]{1,0:T(8,128)S(1)}, f32[12,256]{1,0:T(8,128)}, u32[]{:S(2)}) copy-start(f32[12,256]{1,0:T(8,128)} %get-tuple-element.23) | copy-start | bytes 36868
  94.1 3.2 %copy-start.7 = (bf16[512,12,64]{0,2,1:T(8,128)(2,1)S(1)}, bf16[512,12,64]{0,2,1:T(8,128)(2,1)}, u32[]{:S(2)}) copy-start(bf16[512,12,64]{0,2,1:T(8,128)(2,1)} %fusion.33) | copy-start | bytes 2359300
  94.1 3.3 %copy-start.1 = (bf16[1,256,768]{2,1,0:T(8,128)(2,1)S(1)}, bf16[1,256,768]{2,1,0:T(8,128)(2,1)}, u32[]{:S(2)}) copy-start(bf16[1,256,768]{2,1,0:T(8,128)(2,1)} %param.6) | copy-start | bytes 1179652
  94.1 3.3 %copy-start.10 = (bf16[12,64,256]{2,1,0:T(8,128)(2,1)S(1)}, bf16[12,64,256]{2,1,0:T(8,128)(2,1)}, u32[]{:S(2)}) copy-start(bf16[12,64,256]{2,1,0:T(8,128)(2,1)} %fusion.40) | copy-start | bytes 1179652
  95.4 3.3 %copy-start.3 = (bf16[256,12,64]{0,2,1:T(8,128)(2,1)}, bf16[256,12,64]{0,2,1:T(8,128)(2,1)S(1)}, u32[]{:S(2)}) copy-start(bf16[256,12,64]{0,2,1:T(8,128)(2,1)S(1)} %get-tuple-element.20) | copy-start | bytes 1179652
  97.4 1.4 copy-start.5
  98.8 1.6 copy-start.15
  98.8 1.6 copy-start.18
  112.4 0.7 copy-start.16
  113.0 2.7 %copy-start.4 = (bf16[256,12,64]{0,2,1:T(8,128)(2,1)S(1)}, bf16[256,12,64]{0,2,1:T(8,128)(2,1)}, u32[]{:S(2)}) copy-start(bf16[256,12,64]{0,2,1:T(8,128)(2,1)} %copy-done.3) | copy-start | bytes 1179652
  113.1 2.7 %copy-start.6 = (bf16[256,12,64]{0,2,1:T(8,128)(2,1)S(1)}, bf16[256,12,64]{0,2,1:T(8,128)(2,1)}, u32[]{:S(2)}) copy-start(bf16[256,12,64]{0,2,1:T(8,128)(2,1)} %copy-done.5) | copy-start | bytes 1179652
  113.1 2.7 %copy-start.11 = (bf16[12,64,256]{2,1,0:T(8,128)(2,1)S(1)}, bf16[12,64,256]{2,1,0:T(8,128)(2,1)}, u32[]{:S(2)}) copy-start(bf16[12,64,256]{2,1,0:T(8,128)(2,1)} %fusion.40) | copy-start | bytes 1179652
  113.1 3.1 %copy-start.19 = (bf16[768,2304]{1,0:T(8,128)(2,1)S(1)}, bf16[768,2304]{1,0:T(8,128)(2,1)}, u32[]{:S(2)}) copy-start(bf16[768,2304]{1,0:T(8,128)(2,1)} %param.10) | copy-start | bytes 10616836
Sparse Core Ops, SparseCore 0:
  112.5 113.8 reduce-scatter.1
